TPU v7x, 256 devices: a whole 4x4x8 slice. The times are simulated.
256 devices in a mesh: row: 8 (over y, core), col: 32 (over z, x).
Axes of the slice: x: 4, y: 4, z: 8, core: 2. Of those that a mesh axis runs over, the one named last changes fastest.
Arguments:
- constraint: bfloat16 [16384, 65536], P('row', 'col'), may hold values from -0.0234375 to 0.0234375
- pattern: int32 [128, 512], P('row', 'col'), may hold values 0 or 1
- objective: float32 [65536, 256], P('col'), may hold values from -31 to 31
- row_bound: float32 [16384, 256], P('row'), may hold values from -31 to 31
- lower_bound: float32 [65536], P('col'), may hold values from -2 to -0.5
- upper_bound: float32 [65536], P('col'), may hold values from 0.5 to 2
Outputs:
- primal: float32 [65536, 256], P('col')
- dual_values: float32 [16384, 256], P('row')
- residual_norms: float32 [256], replicated
All inputs are finite; a program needn't handle non-finite values. No bound on the sum of `pattern` on one device may be relied on, other than what follows from the above.
Results may differ from a plain program's by a relative error of at most 0.0019.
Values may be sent and summed in bfloat16 or wider, within the bound.
A program may use at most 128 MiB of HBM per device.

v0:
```python
import functools

import jax
import jax.numpy as jnp
from jax import lax
from jax.sharding import Mesh
from jax.sharding import PartitionSpec as P

BLOCK = 128
ITERS = 3
ROW_COL = ("row_0", "row_1", "col_0", "col_1")
ROW = ("row_0", "row_1")
COL = ("col_0", "col_1")


step_primal = 0.6
step_dual = 0.6
epsilon = 1e-06


def by_axis(array, axes):
    return functools.reduce(lax.psum, axes, array)


def cut_along(array, dim, size):
    before, after = (array.shape[:dim], array.shape[dim + 1 :])
    return jnp.moveaxis(array.reshape(*before, size, -1, *after), dim, 0)


def sum_at_owner(array, axis, dim):
    size = lax.axis_size(axis)
    tiles = lax.all_to_all(cut_along(array, dim, size), axis, 0, 0, tiled=True)
    return jnp.sum(tiles.astype(jnp.float32), axis=0)


def sent_to_all(array, axis):
    copies = jnp.broadcast_to(array, (lax.axis_size(axis), *array.shape))
    return lax.all_to_all(copies, axis, split_axis=0, concat_axis=0, tiled=True)


def laid_out(tiles, dim):
    lengths = list(tiles.shape[1:])
    lengths[dim] *= tiles.shape[0]
    return jnp.moveaxis(tiles, 0, dim).reshape(lengths)


def gathered_copies(array, axis, dim):
    tiles = sent_to_all(array, axis)
    return laid_out(tiles, dim)


def masked(constraint, pattern):
    row_blocks, col_blocks = pattern.shape
    blocks = (
        constraint.reshape(row_blocks, BLOCK, col_blocks, BLOCK)
        * pattern.astype(jnp.bfloat16)[:, None, :, None]
    )
    return blocks.reshape(row_blocks * BLOCK, col_blocks * BLOCK)


def transposed(matrix, values):
    return lax.dot_general(
        matrix, values, (((0,), (0,)), ((), ())), preferred_element_type=jnp.float32
    )


def partial_stats(slack_share, displacement):
    return jnp.stack(
        [jnp.sum(jnp.maximum(slack_share, 0.0) ** 2, axis=0), jnp.sum(displacement**2, axis=0)]
    )


def settle(record):
    return by_axis(record, ROW_COL)


def on_device(constraint, pattern, objective, row_bound, lower_bound, upper_bound):
    matrix = masked(constraint, pattern)
    local_rows, local_cols = matrix.shape
    batch_size = objective.shape[1]
    row_devices = lax.axis_size(ROW)
    col_devices = lax.axis_size(COL)
    total_rows = local_rows * row_devices
    total_cols = local_cols * col_devices
    row_share = local_rows // col_devices
    col_share = local_cols // row_devices
    row_offset = lax.axis_index(COL) * row_share
    col_offset = lax.axis_index(ROW) * col_share
    records = []
    lower_share = lax.dynamic_slice_in_dim(lower_bound, col_offset, col_share, 0)[:, None]
    upper_share = lax.dynamic_slice_in_dim(upper_bound, col_offset, col_share, 0)[:, None]
    objective_share = lax.dynamic_slice_in_dim(objective, col_offset, col_share, 0)
    bound_share = lax.dynamic_slice_in_dim(row_bound, row_offset, row_share, 0)
    primal = jnp.zeros((col_share, batch_size), jnp.float32)
    dual_share = jnp.zeros((row_share, batch_size), jnp.float32)
    dual_full = jnp.zeros((local_rows, batch_size), jnp.bfloat16)
    for iteration in range(ITERS):
        if iteration == 0:
            gradient = objective_share
        else:

            def dual_term(offset, amount, dual_full=dual_full):
                return transposed(matrix, dual_full)

            gradient = objective_share - sum_at_owner(
                dual_term(jnp.int32(0), col_share * lax.axis_size(ROW)).astype(jnp.bfloat16), ROW, 0
            )
        updated = jnp.clip(primal - step_primal * gradient, lower_share, upper_share)
        extrapolated = (2.0 * updated - primal).astype(jnp.bfloat16)
        partial_rows = jnp.dot(
            matrix, gathered_copies(extrapolated, ROW, 0), preferred_element_type=jnp.float32
        )
        product_share = sum_at_owner(partial_rows.astype(jnp.bfloat16), COL, 0)
        slack_share = bound_share - product_share
        dual_share = jnp.maximum(dual_share + step_dual * slack_share, 0.0)
        records.append(settle(partial_stats(slack_share, updated - primal)))
        primal = updated
        if iteration + 1 < ITERS:
            dual_full = gathered_copies(dual_share.astype(jnp.bfloat16), COL, 0)
    primal_out = lax.all_gather(primal, ROW, axis=0, tiled=True)
    dual_out = gathered_copies(dual_share, COL, 0)
    stacked = jnp.stack(records)
    residual_norms = jnp.zeros((batch_size,), jnp.float32)
    for iteration in range(ITERS):
        residual_norms = (
            residual_norms
            + jnp.sqrt(stacked[iteration, 0] / total_rows + epsilon)
            + jnp.sqrt(stacked[iteration, 1] / total_cols + epsilon)
        )
    return (primal_out, dual_out, residual_norms)


def solution(mesh):
    torus = Mesh(mesh.devices.reshape(4, 2, 8, 4), ("row_0", "row_1", "col_0", "col_1"))
    in_specs = (P(ROW, COL), P(ROW, COL), P(COL, None), P(ROW, None), P(COL), P(COL))
    out_specs = (P(COL, None), P(ROW, None), P())
    return jax.shard_map(
        on_device, mesh=torus, in_specs=in_specs, out_specs=out_specs, check_vma=False
    )
```

profile of v0, /device:TPU:8, one launch (start us, length us, event | category | flops | bytes accessed | tf_op | source)
XLA Modules:
  0.0 389.2 jit_solution(3193783697460140228)
XLA Ops:
  10.8 5.6 %all-to-all-start = ((bf16[8,256,256]{2,1,0:T(8,128)(2,1)}), bf16[8,256,256]{2,1,0:T(8,128)(2,1)S(1)}, u32[]{:S(2)}, u32[]{:S(2)}) async-start(bf16[8,256,256]{2,1,0:T(8,128)(2,1)} %broadcast_in_dim.25), calls=%async_computation | async-start | bytes 2097152 | tf_op jit(solution)/shard_map/all_to_all | solution.py:38
  19.9 4.2 %bitcast_multiply_fusion = bf16[2048,2048]{1,0:T(8,128)(2,1)} fusion(bf16[2048,2048]{1,0:T(8,128)(2,1)S(1)} %copy-done, bf16[256,8,16,128]{3,2,1,0:T(8,128)(2,1)S(1)} %bitcast.35), kind=kLoop, calls=%fused_computation | loop fusion | flops 4194304 | bytes 25165824 | tf_op jit(solution)/shard_map/mul | solution.py:55
  24.1 6.9 %all-to-all-done = bf16[8,256,256]{2,1,0:T(8,128)(2,1)S(1)} async-done(((bf16[8,256,256]{2,1,0:T(8,128)(2,1)}), bf16[8,256,256]{2,1,0:T(8,128)(2,1)S(1)}, u32[]{:S(2)}, u32[]{:S(2)}) %all-to-all-start) | async-done | bytes 1048608 | tf_op jit(solution)/shard_map/all_to_all | solution.py:38
  31.0 6.7 %convolution_convert_fusion.4 = bf16[2048,256]{1,0:T(8,128)(2,1)} fusion(bf16[2048,2048]{1,0:T(8,128)(2,1)} %bitcast_multiply_fusion, bf16[2048,256]{1,0:T(8,128)(2,1)S(1)} %bitcast.39), kind=kOutput, calls=%fused_computation.5 | convolution fusion | flops 2148007936 | bytes 10485760 | tf_op jit(solution)/shard_map/dot_general | solution.py:110
  37.7 10.6 %all-to-all-start.1 = ((bf16[32,64,256]{2,1,0:T(8,128)(2,1)}), bf16[32,64,256]{2,1,0:T(8,128)(2,1)S(1)}, u32[]{:S(2)}, u32[]{:S(2)}) async-start(bf16[32,64,256]{2,1,0:T(8,128)(2,1)} %bitcast.1), calls=%async_computation.1 | async-start | bytes 2097152 | tf_op jit(solution)/shard_map/all_to_all | solution.py:32
  48.3 27.7 %all-to-all-done.1 = bf16[32,64,256]{2,1,0:T(8,128)(2,1)S(1)} async-done(((bf16[32,64,256]{2,1,0:T(8,128)(2,1)}), bf16[32,64,256]{2,1,0:T(8,128)(2,1)S(1)}, u32[]{:S(2)}, u32[]{:S(2)}) %all-to-all-start.1) | async-done | bytes 1048608 | tf_op jit(solution)/shard_map/all_to_all | solution.py:32
  77.2 32.4 %all_to_all.55 = bf16[32,64,256]{2,1,0:T(8,128)(2,1)S(1)} all-to-all(bf16[32,64,256]{2,1,0:T(8,128)(2,1)S(1)} %broadcast_in_dim.26), channel_id=1, replica_groups=mesh['row_0'=4,'row_1'=2,'col_0'=8,'col_1'=4] {'col_0','col_1'}, dimensions={0} | all-to-all | bytes 2097152 | tf_op jit(solution)/shard_map/all_to_all | solution.py:38
  109.6 6.1 %convolution_convert_fusion.3 = bf16[2048,256]{1,0:T(8,128)(2,1)S(1)} fusion(bf16[2048,2048]{1,0:T(8,128)(2,1)} %bitcast_multiply_fusion, bf16[2048,256]{1,0:T(8,128)(2,1)S(1)} %bitcast.42), kind=kOutput, calls=%fused_computation.4 | convolution fusion | flops 2148007936 | bytes 10485760 | tf_op jit(solution)/shard_map/dot_general | solution.py:62
  115.6 18.5 %all_to_all.56 = bf16[8,256,256]{2,1,0:T(8,128)(2,1)S(1)} all-to-all(bf16[8,256,256]{2,1,0:T(8,128)(2,1)S(1)} %bitcast.43), channel_id=1, replica_groups=mesh['row_0'=4,'row_1'=2,'col_0'=8,'col_1'=4] {'row_0','row_1'}, dimensions={0} | all-to-all | bytes 2097152 | tf_op jit(solution)/shard_map/all_to_all | solution.py:32
  135.5 18.4 %all_to_all.57 = bf16[8,256,256]{2,1,0:T(8,128)(2,1)S(1)} all-to-all(bf16[8,256,256]{2,1,0:T(8,128)(2,1)S(1)} %broadcast_in_dim.27), channel_id=1, replica_groups=mesh['row_0'=4,'row_1'=2,'col_0'=8,'col_1'=4] {'row_0','row_1'}, dimensions={0} | all-to-all | bytes 2097152 | tf_op jit(solution)/shard_map/all_to_all | solution.py:38
  153.9 2.5 convolution_convert_fusion.2
  156.4 33.1 %all_to_all.58 = bf16[32,64,256]{2,1,0:T(8,128)(2,1)S(1)} all-to-all(bf16[32,64,256]{2,1,0:T(8,128)(2,1)S(1)} %bitcast.45), channel_id=1, replica_groups=mesh['row_0'=4,'row_1'=2,'col_0'=8,'col_1'=4] {'col_0','col_1'}, dimensions={0} | all-to-all | bytes 2097152 | tf_op jit(solution)/shard_map/all_to_all | solution.py:32
  190.6 32.3 %all_to_all.59 = bf16[32,64,256]{2,1,0:T(8,128)(2,1)S(1)} all-to-all(bf16[32,64,256]{2,1,0:T(8,128)(2,1)S(1)} %broadcast_in_dim.28), channel_id=1, replica_groups=mesh['row_0'=4,'row_1'=2,'col_0'=8,'col_1'=4] {'col_0','col_1'}, dimensions={0} | all-to-all | bytes 2097152 | tf_op jit(solution)/shard_map/all_to_all | solution.py:38
  222.9 2.7 convolution_convert_fusion.1
  225.6 18.4 %all_to_all.60 = bf16[8,256,256]{2,1,0:T(8,128)(2,1)S(1)} all-to-all(bf16[8,256,256]{2,1,0:T(8,128)(2,1)S(1)} %bitcast.47), channel_id=1, replica_groups=mesh['row_0'=4,'row_1'=2,'col_0'=8,'col_1'=4] {'row_0','row_1'}, dimensions={0} | all-to-all | bytes 2097152 | tf_op jit(solution)/shard_map/all_to_all | solution.py:32
  245.4 18.4 %all_to_all.61 = bf16[8,256,256]{2,1,0:T(8,128)(2,1)S(1)} all-to-all(bf16[8,256,256]{2,1,0:T(8,128)(2,1)S(1)} %broadcast_in_dim.29), channel_id=1, replica_groups=mesh['row_0'=4,'row_1'=2,'col_0'=8,'col_1'=4] {'row_0','row_1'}, dimensions={0} | all-to-all | bytes 2097152 | tf_op jit(solution)/shard_map/all_to_all | solution.py:38
  263.8 5.7 %convolution_convert_fusion = bf16[2048,256]{1,0:T(8,128)(2,1)S(1)} fusion(bf16[2048,2048]{1,0:T(8,128)(2,1)} %bitcast_multiply_fusion, bf16[2048,256]{1,0:T(8,128)(2,1)S(1)} %bitcast.40), kind=kOutput, calls=%fused_computation.1 | convolution fusion | flops 2148007936 | bytes 10485760 | tf_op jit(solution)/shard_map/dot_general | solution.py:110
  269.5 33.1 %all_to_all.62 = bf16[32,64,256]{2,1,0:T(8,128)(2,1)S(1)} all-to-all(bf16[32,64,256]{2,1,0:T(8,128)(2,1)S(1)} %bitcast.41), channel_id=1, replica_groups=mesh['row_0'=4,'row_1'=2,'col_0'=8,'col_1'=4] {'col_0','col_1'}, dimensions={0} | all-to-all | bytes 2097152 | tf_op jit(solution)/shard_map/all_to_all | solution.py:32
  305.2 5.6 %all-to-all-start.10 = ((f32[32,64,256]{2,1,0:T(8,128)}), f32[32,64,256]{2,1,0:T(8,128)S(1)}, u32[]{:S(2)}, u32[]{:S(2)}) async-start(f32[32,64,256]{2,1,0:T(8,128)} %broadcast_in_dim.30), calls=%async_computation.10 | async-start | bytes 4194304 | tf_op jit(solution)/shard_map/all_to_all | solution.py:38
  311.6 9.2 %all-reduce.2 = (f32[2,256]{1,0:T(2,128)S(1)}, f32[2,256]{1,0:T(2,128)S(1)}, f32[2,256]{1,0:T(2,128)S(1)}) all-reduce(f32[2,256]{1,0:T(2,128)S(1)} %pad_maximum_fusion.2, f32[2,256]{1,0:T(2,128)S(1)} %get-tuple-element.27, f32[2,256]{1,0:T(2,128)S(1)} %get-tuple-element.26), channel_id=1, replica_groups=mesh['row_0'=4,'row_1'=2,'col_0'=8,'col_1'=4] {'row_0'}, use_global_device_ids=true, to_apply=%region_19.20 | all-reduce | flops 1536 | bytes 12288 | tf_op jit(solution)/shard_map/psum | solution.py:22
  320.8 2.5 all-reduce.3
  323.3 44.1 %all-reduce = (f32[2,256]{1,0:T(2,128)S(1)}, f32[2,256]{1,0:T(2,128)S(1)}, f32[2,256]{1,0:T(2,128)S(1)}) all-reduce(f32[2,256]{1,0:T(2,128)S(1)} %get-tuple-element.17, f32[2,256]{1,0:T(2,128)S(1)} %get-tuple-element.18, f32[2,256]{1,0:T(2,128)S(1)} %get-tuple-element.19), channel_id=1, replica_groups=mesh['row_0'=4,'row_1'=2,'col_0'=8,'col_1'=4] {'col_0'}, use_global_device_ids=true, to_apply=%region_21.22 | all-reduce | flops 1536 | bytes 12288 | tf_op jit(solution)/shard_map/psum | solution.py:22
  367.3 10.1 %all-reduce.1 = (f32[1,2,256]{2,1,0:T(2,128)S(1)}, f32[1,2,256]{2,1,0:T(2,128)S(1)}, f32[1,2,256]{2,1,0:T(2,128)S(1)}) all-reduce(f32[1,2,256]{2,1,0:T(2,128)S(1)} %bitcast.54, f32[1,2,256]{2,1,0:T(2,128)S(1)} %bitcast.55, f32[1,2,256]{2,1,0:T(2,128)S(1)} %bitcast.56), channel_id=1, replica_groups=mesh['row_0'=4,'row_1'=2,'col_0'=8,'col_1'=4] {'col_1'}, use_global_device_ids=true, to_apply=%region_22.23 | all-reduce | flops 1536 | bytes 12288 | tf_op jit(solution)/shard_map/psum | solution.py:22
  378.0 3.0 copy.13
  (42 shorter events, 17.3 us)
Async XLA Ops:
  7.2 9.3 %copy-start.2 = (s32[16,16]{1,0:T(8,128)S(1)}, s32[16,16]{1,0:T(8,128)}, u32[]{:S(2)}) copy-start(s32[16,16]{1,0:T(8,128)} %param.7) | copy-start | bytes 3076
  10.8 20.1 %all-to-all-start = ((bf16[8,256,256]{2,1,0:T(8,128)(2,1)}), bf16[8,256,256]{2,1,0:T(8,128)(2,1)S(1)}, u32[]{:S(2)}, u32[]{:S(2)}) async-start(bf16[8,256,256]{2,1,0:T(8,128)(2,1)} %broadcast_in_dim.25), calls=%async_computation | async-start | bytes 2097152 | tf_op jit(solution)/shard_map/all_to_all | solution.py:38
  16.5 3.4 copy-start
  37.7 38.3 %all-to-all-start.1 = ((bf16[32,64,256]{2,1,0:T(8,128)(2,1)}), bf16[32,64,256]{2,1,0:T(8,128)(2,1)S(1)}, u32[]{:S(2)}, u32[]{:S(2)}) async-start(bf16[32,64,256]{2,1,0:T(8,128)(2,1)} %bitcast.1), calls=%async_computation.1 | async-start | bytes 2097152 | tf_op jit(solution)/shard_map/all_to_all | solution.py:32
  77.2 76.7 %slice-start = ((s8[8388608]{0:T(1024)(128)(4,1)}), s8[4194304]{0:T(1024)(128)(4,1)S(1)}, s32[]{:S(2)}) async-start(s8[8388608]{0:T(1024)(128)(4,1)} %bitcast.36), calls=%async_computation.12 | async-start | bytes 8388608
  109.6 44.3 %slice-start.1 = ((s8[8388608]{0:T(1024)(128)(4,1)}), s8[4194304]{0:T(1024)(128)(4,1)S(1)}, s32[]{:S(2)}) async-start(s8[8388608]{0:T(1024)(128)(4,1)} %bitcast.36), calls=%async_computation.13 | async-start | bytes 8388608
  245.3 24.3 %copy-start.1 = (f32[256,256]{1,0:T(8,128)}, f32[256,256]{1,0:T(8,128)S(1)}, u32[]{:S(2)}) copy-start(f32[256,256]{1,0:T(8,128)S(1)} %get-tuple-element.22) | copy-start | bytes 786436
  305.2 72.8 %all-to-all-start.10 = ((f32[32,64,256]{2,1,0:T(8,128)}), f32[32,64,256]{2,1,0:T(8,128)S(1)}, u32[]{:S(2)}, u32[]{:S(2)}) async-start(f32[32,64,256]{2,1,0:T(8,128)} %broadcast_in_dim.30), calls=%async_computation.10 | async-start | bytes 4194304 | tf_op jit(solution)/shard_map/all_to_all | solution.py:38
  310.8 67.2 %all-gather.2.cloned.1.call-start = ((), (), s32[]{:S(2)}) async-start(), calls=%async_computation.11 | async-start | bytes 2359296 | tf_op jit(solution)/shard_map/all_gather | solution.py:120
Sparse Core Ops, SparseCore 0:
  314.0 26.7 all-gather.1
where the time goes:
time: 390 us; the launch traced here: 389 us
  blocking collectives  270 us (69%)
  waiting for transfers between devices  35.3 us (9%)
  matrix products  23.6 us (6%)
  starting transfers between devices  21.8 us (6%)
  between operations  14.2 us (4%)
  local copies, waits for them, and re-layouts  12.2 us (3%)
  other arithmetic  11.6 us (3%)
    all_to_all x4, blocking collectives, sum_at_owner(): tiles = lax.all_to_all(cut_along(array, dim, size), axis, 0, 0, tiled=True)  103 us
    all_to_all x4, blocking collectives, sent_to_all(): return lax.all_to_all(copies, axis, split_axis=0, concat_axis=0, tiled=True)  102 us
    psum x4, blocking collectives, by_axis(): return functools.reduce(lax.psum, axes, array)  65.8 us
    all_to_all x1, waiting for transfers between devices, sum_at_owner(): tiles = lax.all_to_all(cut_along(array, dim, size), axis, 0, 0, tiled=True)  27.7 us
    dot_general x3, matrix products, on_device(): jnp.dot(matrix, gathered_copies(extrapolated, ROW, 0), preferred_element_...  14.9 us
    all_to_all x2, starting transfers between devices, sent_to_all(): return lax.all_to_all(copies, axis, split_axis=0, concat_axis=0, tiled=True)  11.2 us
    all_to_all x1, starting transfers between devices, sum_at_owner(): tiles = lax.all_to_all(cut_along(array, dim, size), axis, 0, 0, tiled=True)  10.6 us
    dot_general x2, matrix products, transposed(): lax.dot_general(matrix, values, (((0,), (0,)), ((), ())), preferred_eleme...  8.71 us
  transfers between devices with their start and end apart: 4, of which 2 were waited for; matrix products, arithmetic and copies ran while one was open for 2% of the time, Pallas kernels for 0%

commit v1 on v0

v1 whole, which is shorter than its diff:
```python
import functools

import jax
import jax.numpy as jnp
from jax import lax
from jax.experimental import pallas as pl
from jax.experimental.pallas import tpu as pltpu
from jax.sharding import Mesh
from jax.sharding import PartitionSpec as P

MESH = pl.DeviceIdType.MESH
BF16 = jnp.bfloat16
F32 = jnp.float32
BLOCK = 128
ITERS = 3
NY, NC, NZ, NX = 4, 2, 8, 4
ROW = ("y", "c")
COL = ("z", "x")
K = 256
S = 64
HALF = S // 2
GROUP = NX * S
NJ = 4
step_primal = 0.6
step_dual = 0.6
epsilon = 1e-6


def aligned(index, size):
    return pl.ds(pl.multiple_of(index * size, size), size)


def folded(values):
    return jnp.sum(values.reshape(-1, 8, values.shape[-1]), axis=0)


class Ring:
    def __init__(self, axis, groups, from_prev, from_next, half_prev, half_next, sems):
        self.axis, self.groups = axis, groups
        self.me = lax.axis_index(axis)
        self.next = (self.me + 1) % 4
        self.prev = (self.me + 3) % 4
        self.far = (self.me + 2) % 4
        self.from_prev, self.from_next = from_prev, from_next
        self.half_prev, self.half_next = half_prev, half_next
        self.send_sem, self.half_prev_sem, self.half_next_sem, self.prev_sem, self.next_sem, self.gather_sem, self.gather_send = sems

    def copy(self, src, dst, send, recv, to):
        pltpu.make_async_remote_copy(
            src_ref=src, dst_ref=dst, send_sem=send, recv_sem=recv, device_id={self.axis: to}, device_id_type=MESH
        ).start()

    def begin(self, part, s):
        low, high = pl.ds(0, HALF), pl.ds(HALF, HALF)
        self.copy(part.at[s, self.far, low], self.half_prev.at[s], self.send_sem, self.half_prev_sem.at[s], self.next)
        self.copy(part.at[s, self.far, high], self.half_next.at[s], self.send_sem, self.half_next_sem.at[s], self.prev)
        self.copy(part.at[s, self.next, high], self.from_prev.at[s, high], self.send_sem, self.prev_sem.at[s], self.next)
        self.copy(part.at[s, self.prev, low], self.from_next.at[s, low], self.send_sem, self.next_sem.at[s], self.prev)

    def relay(self, part, s):
        low, high = pl.ds(0, HALF), pl.ds(HALF, HALF)
        arrived(self.half_prev.at[s], self.half_prev_sem.at[s])
        part[s, self.next, low] = (part[s, self.next, low].astype(F32) + self.half_prev[s].astype(F32)).astype(BF16)
        self.copy(part.at[s, self.next, low], self.from_prev.at[s, low], self.send_sem, self.prev_sem.at[s], self.next)
        arrived(self.half_next.at[s], self.half_next_sem.at[s])
        part[s, self.prev, high] = (part[s, self.prev, high].astype(F32) + self.half_next[s].astype(F32)).astype(BF16)
        self.copy(part.at[s, self.prev, high], self.from_next.at[s, high], self.send_sem, self.next_sem.at[s], self.prev)

    def total(self, part, s):
        arrived(self.from_prev.at[s], self.prev_sem.at[s])
        arrived(self.from_next.at[s], self.next_sem.at[s])
        return part[s, self.me].astype(F32) + self.from_prev[s].astype(F32) + self.from_next[s].astype(F32)

    def gather_begin(self, piece, s):
        low, high = pl.ds(0, HALF), pl.ds(HALF, HALF)
        mine = piece(s, self.me)
        self.copy(mine.at[low], mine.at[low], self.gather_send, self.gather_sem.at[0, s], self.next)
        self.copy(mine.at[high], mine.at[high], self.gather_send, self.gather_sem.at[1, s], self.prev)
        self.copy(mine.at[high], mine.at[high], self.gather_send, self.gather_sem.at[2, s], self.next)
        self.copy(mine.at[low], mine.at[low], self.gather_send, self.gather_sem.at[3, s], self.prev)

    def gather_relay(self, piece, s):
        low, high = pl.ds(0, HALF), pl.ds(HALF, HALF)
        left, right = piece(s, self.prev), piece(s, self.next)
        arrived(left.at[low], self.gather_sem.at[0, s])
        self.copy(left.at[low], left.at[low], self.gather_send, self.gather_sem.at[4, s], self.next)
        arrived(right.at[high], self.gather_sem.at[1, s])
        self.copy(right.at[high], right.at[high], self.gather_send, self.gather_sem.at[5, s], self.prev)

    def gather_end(self, piece, s):
        low, high = pl.ds(0, HALF), pl.ds(HALF, HALF)
        left, right, far = piece(s, self.prev), piece(s, self.next), piece(s, self.far)
        arrived(left.at[high], self.gather_sem.at[2, s])
        arrived(right.at[low], self.gather_sem.at[3, s])
        arrived(far.at[low], self.gather_sem.at[4, s])
        arrived(far.at[high], self.gather_sem.at[5, s])

    def drain_sum(self, part):
        view = part.at[:, pl.ds(0, 3)]
        arrived(view, self.send_sem)

    def drain_gather(self, part):
        view = part.at[:, pl.ds(0, 3)]
        arrived(view, self.gather_send)


def arrived(ref, sem):
    pltpu.make_async_copy(ref, ref, sem).wait()


SCRATCH = dict(
    matrix=pltpu.VMEM((2048, 2048), BF16),
    turned=pltpu.VMEM((2048, 2048), BF16),
    objective=pltpu.VMEM((2048, K), F32),
    bound=pltpu.VMEM((2048, K), F32),
    primal=pltpu.VMEM((2048, K), F32),
    dual=pltpu.VMEM((2048, K), F32),
    extra=pltpu.VMEM((2048, K), BF16),
    dual_bf=pltpu.VMEM((2048, K), BF16),
    lower=pltpu.VMEM((2048, BLOCK), F32),
    upper=pltpu.VMEM((2048, BLOCK), F32),
    part_x=pltpu.VMEM((NZ, NX, S, K), BF16),
    x_from_prev=pltpu.VMEM((3, NZ, S, K), BF16),
    x_from_next=pltpu.VMEM((3, NZ, S, K), BF16),
    x_half_prev=pltpu.VMEM((3, NZ, HALF, K), BF16),
    x_half_next=pltpu.VMEM((3, NZ, HALF, K), BF16),
    z_send=pltpu.VMEM((NZ, S, K), BF16),
    z_recv=pltpu.VMEM((3, NZ, S, K), BF16),
    share=pltpu.VMEM((S, K), F32),
    rows=pltpu.VMEM((3, NZ, NX, S, K), BF16),
    core_send=pltpu.VMEM((NJ, NY, S, K), BF16),
    core_own=pltpu.VMEM((NJ, NY, S, K), F32),
    core_recv=pltpu.VMEM((2, NJ, NY, S, K), BF16),
    part_y=pltpu.VMEM((NJ, NY, S, K), BF16),
    y_from_prev=pltpu.VMEM((2, NJ, S, K), BF16),
    y_from_next=pltpu.VMEM((2, NJ, S, K), BF16),
    y_half_prev=pltpu.VMEM((2, NJ, HALF, K), BF16),
    y_half_next=pltpu.VMEM((2, NJ, HALF, K), BF16),
    cols=pltpu.VMEM((2, NJ, NC, NY, S, K), BF16),
    violation=pltpu.VMEM((3, 8, K), F32),
    movement=pltpu.VMEM((3, 8, K), F32),
    violation_own=pltpu.VMEM((8, K), F32),
    violation_pair=pltpu.VMEM((8, K), F32),
    violation_core=pltpu.VMEM((8, K), F32),
    violation_y=pltpu.VMEM((4, 8, K), F32),
    movement_own=pltpu.VMEM((8, K), F32),
    movement_row=pltpu.VMEM((8, K), F32),
    movement_x=pltpu.VMEM((4, 8, K), F32),
    movement_z=pltpu.VMEM((8, 8, K), F32),
    load_sem=pltpu.SemaphoreType.DMA((16,)),
    out_sem=pltpu.SemaphoreType.DMA((2,)),
    x_send_sem=pltpu.SemaphoreType.DMA((3,)),
    x_half_prev_sem=pltpu.SemaphoreType.DMA((3, NZ)),
    x_half_next_sem=pltpu.SemaphoreType.DMA((3, NZ)),
    x_prev_sem=pltpu.SemaphoreType.DMA((3, NZ)),
    x_next_sem=pltpu.SemaphoreType.DMA((3, NZ)),
    x_gather_sem=pltpu.SemaphoreType.DMA((3, 6, NZ)),
    x_gather_send=pltpu.SemaphoreType.DMA((3,)),
    z_send_sem=pltpu.SemaphoreType.DMA((3,)),
    z_recv_sem=pltpu.SemaphoreType.DMA((3, NZ)),
    z_gather_send=pltpu.SemaphoreType.DMA((3,)),
    z_gather_sem=pltpu.SemaphoreType.DMA((3, NZ)),
    core_send_sem=pltpu.SemaphoreType.DMA((2,)),
    core_recv_sem=pltpu.SemaphoreType.DMA((2, NJ)),
    core_gather_send=pltpu.SemaphoreType.DMA((2,)),
    core_gather_sem=pltpu.SemaphoreType.DMA((2, NJ)),
    y_send_sem=pltpu.SemaphoreType.DMA((2,)),
    y_half_prev_sem=pltpu.SemaphoreType.DMA((2, NJ)),
    y_half_next_sem=pltpu.SemaphoreType.DMA((2, NJ)),
    y_prev_sem=pltpu.SemaphoreType.DMA((2, NJ)),
    y_next_sem=pltpu.SemaphoreType.DMA((2, NJ)),
    y_gather_sem=pltpu.SemaphoreType.DMA((2, 6, NJ)),
    y_gather_send=pltpu.SemaphoreType.DMA((2,)),
    stat_send_sem=pltpu.SemaphoreType.DMA((4,)),
    stat_x_sem=pltpu.SemaphoreType.DMA((4,)),
    stat_z_sem=pltpu.SemaphoreType.DMA((8,)),
    stat_y_sem=pltpu.SemaphoreType.DMA((4,)),
    stat_c_sem=pltpu.SemaphoreType.DMA((1,)),
)


class Box:
    pass


def kernel(constraint, pattern, objective, row_bound, lower, upper, primal_out, dual_out, norms, *refs):
    b = Box()
    b.__dict__.update(zip(SCRATCH, refs))
    y, c, z, x = (lax.axis_index(name) for name in ("y", "c", "z", "x"))
    other = 1 - c

    barrier = pltpu.get_barrier_semaphore()
    peers = 0
    for name, size, me in (("y", NY, y), ("c", NC, c), ("z", NZ, z), ("x", NX, x)):
        for step in range(1, size):
            pl.semaphore_signal(barrier, inc=1, device_id={name: (me + step) % size}, device_id_type=MESH)
            peers += 1

    def z_target(s):
        return (z + jnp.where(s % 2 == 1, 4 - (s + 1) // 2, 4 + s // 2)) % NZ

    def z_source(s):
        return (z + jnp.where(s % 2 == 1, (s + 1) // 2, NZ - s // 2)) % NZ

    load_objective = pltpu.make_async_copy(objective, b.objective, b.load_sem.at[8])
    load_objective.start()

    def load_matrix(s):
        group = aligned(z_target(s), GROUP)
        return pltpu.make_async_copy(constraint.at[group], b.matrix.at[group], b.load_sem.at[s])

    for s in range(NZ):
        load_matrix(s).start()
    load_bound = pltpu.make_async_copy(row_bound, b.bound, b.load_sem.at[9])
    load_bound.start()

    def spread(i, carry):
        at = aligned(i, BLOCK)
        b.lower[at] = jnp.broadcast_to(lower[pl.ds(i, 1)], (BLOCK, BLOCK)).T
        b.upper[at] = jnp.broadcast_to(upper[pl.ds(i, 1)], (BLOCK, BLOCK)).T
        return carry

    lax.fori_loop(0, 16, spread, 0)

    def wide(values):
        return jnp.concatenate([values, values], axis=1)

    def new_primal(at, gradient, it):
        low, high = wide(b.lower[at]), wide(b.upper[at])
        if it == 0:
            updated = jnp.clip(-step_primal * gradient, low, high)
            moved = updated
            b.extra[at] = (2.0 * updated).astype(BF16)
        else:
            before = b.primal[at]
            updated = jnp.clip(before - step_primal * gradient, low, high)
            moved = updated - before
            b.extra[at] = (2.0 * updated - before).astype(BF16)
        b.primal[at] = updated
        b.movement[it] += folded(moved * moved)

    b.movement[...] = jnp.zeros_like(b.movement)
    b.violation[...] = jnp.zeros_like(b.violation)

    load_objective.wait()

    def first(i, carry):
        at = aligned(i, GROUP)
        new_primal(at, b.objective[at], 0)
        return carry

    lax.fori_loop(0, 8, first, 0)

    def mask_group(group):
        for h in range(2):
            at = aligned(group * 2 + h, BLOCK)
            for j in range(16):
                keep = pattern[group * 2 + h, j].astype(F32).astype(BF16)
                cols = pl.ds(j * BLOCK, BLOCK)
                b.matrix[at, cols] = b.matrix[at, cols] * keep

    def turn_group(group):
        eye = jnp.where(
            lax.broadcasted_iota(jnp.int32, (256, 256), 0) == lax.broadcasted_iota(jnp.int32, (256, 256), 1), 1.0, 0.0
        ).astype(BF16)
        at = aligned(group, GROUP)
        for j in range(8):
            cols = pl.ds(j * 256, 256)
            b.turned[cols, at] = lax.dot_general(
                eye, b.matrix[at, cols], (((1,), (1,)), ((), ())), preferred_element_type=F32
            ).astype(BF16)

    def column_sum(it):
        ring = Ring(
            "x", NZ, b.x_from_prev.at[it], b.x_from_next.at[it], b.x_half_prev.at[it], b.x_half_next.at[it],
            (b.x_send_sem.at[it], b.x_half_prev_sem.at[it], b.x_half_next_sem.at[it], b.x_prev_sem.at[it],
             b.x_next_sem.at[it], b.x_gather_sem.at[it], b.x_gather_send.at[it]),
        )
        rows = b.rows.at[it]

        def piece(group, owner):
            return rows.at[group, owner]

        def z_copy(s):
            return pltpu.make_async_remote_copy(
                src_ref=b.z_send.at[s], dst_ref=b.z_recv.at[it, s], send_sem=b.z_send_sem.at[it],
                recv_sem=b.z_recv_sem.at[it, s], device_id={"z": z_target(s)}, device_id_type=MESH,
            )

        def summing(t, carry):
            @pl.when(t < NZ)
            def _():
                group = z_target(t)
                if it == 0:
                    load_matrix(t).wait()
                    mask_group(group)
                product = jnp.dot(b.matrix[aligned(group, GROUP)], b.extra[...], preferred_element_type=F32)
                b.part_x[t] = product.astype(BF16).reshape(NX, S, K)
                ring.begin(b.part_x, t)
                if it == 0:
                    turn_group(group)

            @pl.when((t >= 2) & (t < NZ + 2))
            def _():
                ring.relay(b.part_x, t - 2)

            @pl.when(t >= 4)
            def _():
                s = t - 4
                total = ring.total(b.part_x, s)

                @pl.when(s < NZ - 1)
                def _():
                    b.z_send[s] = total.astype(BF16)
                    z_copy(s).start()

                @pl.when(s == NZ - 1)
                def _():
                    b.share[...] = total

            return carry

        lax.fori_loop(0, NZ + 4, summing, 0)

        def adding(s, carry):
            arrived(b.z_recv.at[it, s], b.z_recv_sem.at[it, s])
            b.share[...] += b.z_recv[it, s].astype(F32)
            return carry

        lax.fori_loop(0, NZ - 1, adding, 0)
        rows[z, x] = b.share[...].astype(BF16)

        def z_spread(s, carry):
            to = z_source(s)
            mine = piece(z, x)
            pltpu.make_async_remote_copy(
                src_ref=mine, dst_ref=mine, send_sem=b.z_gather_send.at[it], recv_sem=b.z_gather_sem.at[it, z],
                device_id={"z": to}, device_id_type=MESH,
            ).start()
            return carry

        lax.fori_loop(1, NZ, z_spread, 0)

        if it == 0:
            load_bound.wait()

        def gathering(t, carry):
            @pl.when(t < NZ)
            def _():
                group = z_source(t)

                @pl.when(t > 0)
                def _():
                    arrived(piece(group, x), b.z_gather_sem.at[it, group])

                ring.gather_begin(piece, group)

            @pl.when((t >= 2) & (t < NZ + 2))
            def _():
                ring.gather_relay(piece, z_source(t - 2))

            @pl.when(t >= 4)
            def _():
                group = z_source(t - 4)
                ring.gather_end(piece, group)
                at = aligned(group, GROUP)
                slack = b.bound[at] - rows[group].reshape(GROUP, K).astype(F32)
                over = jnp.maximum(slack, 0.0)
                b.violation[it] += folded(over * over)
                if it == 0:
                    dual = jnp.maximum(step_dual * slack, 0.0)
                else:
                    dual = jnp.maximum(b.dual[at] + step_dual * slack, 0.0)
                b.dual[at] = dual
                if it < ITERS - 1:
                    b.dual_bf[at] = dual.astype(BF16)
                else:
                    pltpu.make_async_copy(b.dual.at[at], dual_out.at[at], b.out_sem.at[1]).start()

            return carry

        lax.fori_loop(0, NZ + 4, gathering, 0)
        ring.drain_sum(b.part_x)
        ring.drain_gather(b.part_x)
        arrived(b.z_send.at[pl.ds(0, NZ - 1)], b.z_send_sem.at[it])
        arrived(b.z_send.at[pl.ds(0, NZ - 1)], b.z_gather_send.at[it])

    def row_sum(it):
        n = it - 1
        ring = Ring(
            "y", NJ, b.y_from_prev.at[n], b.y_from_next.at[n], b.y_half_prev.at[n], b.y_half_next.at[n],
            (b.y_send_sem.at[n], b.y_half_prev_sem.at[n], b.y_half_next_sem.at[n], b.y_prev_sem.at[n],
             b.y_next_sem.at[n], b.y_gather_sem.at[n], b.y_gather_send.at[n]),
        )
        cols = b.cols.at[n]

        def piece(j, owner):
            return cols.at[j, c, owner]

        def swap(src, dst, send, recv):
            pltpu.make_async_remote_copy(
                src_ref=src, dst_ref=dst, send_sem=send, recv_sem=recv, device_id={"c": other}, device_id_type=MESH
            ).start()

        def product(j, core):
            return jnp.dot(b.turned[aligned(j * 2 + core, GROUP)], b.dual_bf[...], preferred_element_type=F32)

        def update(j, core):
            at = aligned(j * 2 + core, GROUP)
            new_primal(at, b.objective[at] - cols[j, core].reshape(GROUP, K).astype(F32), it)

        def body(t, carry):
            @pl.when(t < NJ)
            def _():
                b.core_send[t] = product(t, other).astype(BF16).reshape(NY, S, K)
                swap(b.core_send.at[t], b.core_recv.at[n, t], b.core_send_sem.at[n], b.core_recv_sem.at[n, t])
                b.core_own[t] = product(t, c).reshape(NY, S, K)

            @pl.when((t >= 1) & (t < NJ + 1))
            def _():
                j = t - 1
                arrived(b.core_recv.at[n, j], b.core_recv_sem.at[n, j])
                b.part_y[j] = (b.core_own[j] + b.core_recv[n, j].astype(F32)).astype(BF16)
                ring.begin(b.part_y, j)

            @pl.when((t >= 3) & (t < NJ + 3))
            def _():
                ring.relay(b.part_y, t - 3)

            @pl.when((t >= 5) & (t < NJ + 5))
            def _():
                j = t - 5
                cols[j, c, y] = ring.total(b.part_y, j).astype(BF16)
                ring.gather_begin(piece, j)

            @pl.when((t >= 7) & (t < NJ + 7))
            def _():
                ring.gather_relay(piece, t - 7)

            @pl.when((t >= 9) & (t < NJ + 9))
            def _():
                j = t - 9
                ring.gather_end(piece, j)
                swap(cols.at[j, c], cols.at[j, c], b.core_gather_send.at[n], b.core_gather_sem.at[n, j])
                update(j, c)

            @pl.when(t >= 10)
            def _():
                j = t - 10
                arrived(cols.at[j, other], b.core_gather_sem.at[n, j])
                update(j, other)

            return carry

        lax.fori_loop(0, NJ + 10, body, 0)
        ring.drain_sum(b.part_y)
        ring.drain_gather(b.part_y)
        arrived(b.core_send, b.core_send_sem.at[n])
        arrived(b.core_send, b.core_gather_send.at[n])

    def stat_copy(src, dst, send, recv, to):
        pltpu.make_async_remote_copy(
            src_ref=src, dst_ref=dst, send_sem=b.stat_send_sem.at[send], recv_sem=recv, device_id=to, device_id_type=MESH
        ).start()

    def three_rows(parts):
        sums = [jnp.sum(parts[i], axis=0, keepdims=True) for i in range(3)]
        return jnp.concatenate(sums + [jnp.zeros((5, K), F32)], axis=0)

    pl.semaphore_wait(barrier, peers)
    column_sum(0)
    row_sum(1)
    column_sum(1)
    row_sum(2)

    save_primal = pltpu.make_async_copy(b.primal, primal_out, b.out_sem.at[0])
    save_primal.start()
    b.movement_own[...] = three_rows(b.movement)
    for step in range(1, NX):
        stat_copy(b.movement_own, b.movement_x.at[step], 0, b.stat_x_sem.at[step], {"x": (x + step) % NX})

    column_sum(2)

    b.violation_own[...] = three_rows(b.violation)
    stat_copy(b.violation_own, b.violation_core, 2, b.stat_c_sem.at[0], {"c": other})
    row = b.movement_own[...]
    for step in range(1, NX):
        arrived(b.movement_x.at[step], b.stat_x_sem.at[step])
        row += b.movement_x[step]
    b.movement_row[...] = row
    for step in range(1, NZ):
        stat_copy(b.movement_row, b.movement_z.at[step], 1, b.stat_z_sem.at[step], {"z": (z + step) % NZ})
    arrived(b.violation_core, b.stat_c_sem.at[0])
    pair = b.violation_own[...] + b.violation_core[...]
    b.violation_pair[...] = pair
    for step in range(1, NY):
        stat_copy(b.violation_pair, b.violation_y.at[step], 3, b.stat_y_sem.at[step], {"y": (y + step) % NY})

    moved = b.movement_row[...]
    for step in range(1, NZ):
        arrived(b.movement_z.at[step], b.stat_z_sem.at[step])
        moved += b.movement_z[step]
    for step in range(1, NY):
        arrived(b.violation_y.at[step], b.stat_y_sem.at[step])
        pair += b.violation_y[step]
    each = jnp.sqrt(pair / (2048 * NY * NC) + epsilon) + jnp.sqrt(moved / (2048 * NZ * NX) + epsilon)
    norms[...] = each[0:1] + each[1:2] + each[2:3]

    arrived(b.movement_x.at[pl.ds(1, 3)], b.stat_send_sem.at[0])
    arrived(b.movement_z.at[pl.ds(1, 7)], b.stat_send_sem.at[1])
    arrived(b.violation_core, b.stat_send_sem.at[2])
    arrived(b.violation_y.at[pl.ds(1, 3)], b.stat_send_sem.at[3])
    save_primal.wait()
    arrived(b.dual, b.out_sem.at[1])


def on_device(constraint, pattern, objective, row_bound, lower_bound, upper_bound):
    primal, dual, norms = pl.pallas_call(
        kernel,
        out_shape=(
            jax.ShapeDtypeStruct((2048, K), F32),
            jax.ShapeDtypeStruct((2048, K), F32),
            jax.ShapeDtypeStruct((1, K), F32),
        ),
        in_specs=[
            pl.BlockSpec(memory_space=pl.ANY),
            pl.BlockSpec(memory_space=pltpu.SMEM),
            pl.BlockSpec(memory_space=pl.ANY),
            pl.BlockSpec(memory_space=pl.ANY),
            pl.BlockSpec(memory_space=pltpu.VMEM),
            pl.BlockSpec(memory_space=pltpu.VMEM),
        ],
        out_specs=(
            pl.BlockSpec(memory_space=pl.ANY),
            pl.BlockSpec(memory_space=pl.ANY),
            pl.BlockSpec(memory_space=pltpu.VMEM),
        ),
        scratch_shapes=list(SCRATCH.values()),
        compiler_params=pltpu.CompilerParams(
            collective_id=0, has_side_effects=True, vmem_limit_bytes=62 * 1024 * 1024
        ),
        name="pdhg",
    )(constraint, pattern, objective, row_bound, lower_bound.reshape(16, BLOCK), upper_bound.reshape(16, BLOCK))
    return primal, dual, norms.reshape(K)


def solution(mesh):
    torus = Mesh(mesh.devices.reshape(NY, NC, NZ, NX), ("y", "c", "z", "x"))
    in_specs = (P(ROW, COL), P(ROW, COL), P(COL, None), P(ROW, None), P(COL), P(COL))
    out_specs = (P(COL, None), P(ROW, None), P())
    return jax.shard_map(on_device, mesh=torus, in_specs=in_specs, out_specs=out_specs, check_vma=False)
```

time: 390 us -> 183 us (0.47)
  blocking collectives: 270 us -> 0 us
  Pallas kernels: 0 us -> 175 us
  waiting for transfers between devices: 35.3 us -> 0 us
  matrix products: 23.6 us -> 0 us
  starting transfers between devices: 21.8 us -> 0 us
  between operations: 14.2 us -> 0.65 us
  other arithmetic: 11.6 us -> 0 us
  local copies, waits for them, and re-layouts: 12.2 us -> 5.08 us
    all_to_all x8 -> x0, blocking collectives: 205 us -> none  [the longest x4 103 us: sum_at_owner(): tiles = lax.all_to_all(cut_along(array, dim, size), axis, 0, 0, tiled=True)]
    pallas_call x0 -> x1, Pallas kernels: none -> 175 us  [on_device(): pl.pallas_call(kernel, out_shape=(jax.ShapeDtypeStruct((2048, K), F32), j...]
    psum x4 -> x0, blocking collectives: 65.8 us -> none  [by_axis(): return functools.reduce(lax.psum, axes, array)]
    all_to_all x3 -> x0, waiting for transfers between devices: 34.6 us -> none  [the longest x1 27.7 us: sum_at_owner(): tiles = lax.all_to_all(cut_along(array, dim, size), axis, 0, 0, tiled=True)]
    dot_general x5 -> x0, matrix products: 23.6 us -> none  [the longest x3 14.9 us: on_device(): jnp.dot(matrix, gathered_copies(extrapolated, ROW, 0), preferred_element_...]
    all_to_all x3 -> x0, starting transfers between devices: 21.8 us -> none  [the longest x2 11.2 us: sent_to_all(): return lax.all_to_all(copies, axis, split_axis=0, concat_axis=0, tiled=True)]
    mul x1 -> x0, other arithmetic: 4.23 us -> none  [masked(): constraint.reshape(row_blocks, BLOCK, col_blocks, BLOCK)]
  transfers between devices with their start and end apart: 4 -> 0, of which waited for: 2 -> 0; matrix products, arithmetic and copies ran while one was open for 2% -> 0% of each run, Pallas kernels for 0% -> 0%
where the time goes in v1:
time: 183 us; the launch traced here: 181 us
  Pallas kernels  175 us (96%)
  local copies, waits for them, and re-layouts  5.08 us (3%)
    pallas_call x1, Pallas kernels, on_device(): pl.pallas_call(kernel, out_shape=(jax.ShapeDtypeStruct((2048, K), F32), j...  175 us
    unnamed x7, local copies, waits for them, and re-layouts  5.08 us

profile of v1, /device:TPU:8, one launch (start us, length us, event | category | flops | bytes accessed | tf_op | source)
XLA Modules:
  0.0 180.8 jit_solution(15642332944239187177)
XLA Ops:
  0.6 175.1 %pdhg.1 = (f32[2048,256]{1,0:T(8,128)}, f32[2048,256]{1,0:T(8,128)}, f32[1,256]{1,0:T(1,128)}) custom-call(bf16[2048,2048]{1,0:T(8,128)(2,1)} %constraint.1, s32[16,16]{1,0:T(8,128)} %pattern.1, f32[2048,256]{1,0:T(8,128)} %objective.1, f32[2048,256]{1,0:T(8,128)} %row_bound.1, f32[16,128]{1,0:T(8,128)} %bitcast.3, f32[16,128]{1,0:T(8,128)} %bitcast.4), custom_call_target="tpu_custom_call" | custom-call | tf_op jit(solution)/shard_map/pdhg/pallas_call | solution.py:518
  175.7 0.0 copy-start
  175.7 3.2 %copy.12 = f32[2048,256]{1,0:T(8,128)} copy(f32[2048,256]{1,0:T(8,128)} %get-tuple-element.12) | data formatting | bytes 4194304
  178.9 0.0 copy-done
  178.9 0.0 copy-start.1
  178.9 1.3 copy.13
  180.2 0.0 copy-done.1
  180.2 0.6 copy.14
Async XLA Ops:
  175.7 3.2 %copy-start = (f32[2048,256]{1,0:T(8,128)S(1)}, f32[2048,256]{1,0:T(8,128)}, u32[]{:S(2)}) copy-start(f32[2048,256]{1,0:T(8,128)} %get-tuple-element.13) | copy-start | bytes 6291460
  178.9 1.3 copy-start.1

commit v2 on v1

--- a/solution.py
+++ b/solution.py
@@ -21,6 +21,11 @@
 HALF = S // 2
 GROUP = NX * S
 NJ = 4
+LS = 4
+LG = 4
+LR = 3
+FAR_X = 6
+FAR_Y = 3
 step_primal = 0.6
 step_dual = 0.6
 epsilon = 1e-6
@@ -71,7 +76,7 @@
         arrived(self.from_next.at[s], self.next_sem.at[s])
         return part[s, self.me].astype(F32) + self.from_prev[s].astype(F32) + self.from_next[s].astype(F32)
 
-    def gather_begin(self, piece, s):
+    def gather_begin(self, piece, s, direct):
         low, high = pl.ds(0, HALF), pl.ds(HALF, HALF)
         mine = piece(s, self.me)
         self.copy(mine.at[low], mine.at[low], self.gather_send, self.gather_sem.at[0, s], self.next)
@@ -79,13 +84,25 @@
         self.copy(mine.at[high], mine.at[high], self.gather_send, self.gather_sem.at[2, s], self.next)
         self.copy(mine.at[low], mine.at[low], self.gather_send, self.gather_sem.at[3, s], self.prev)
 
-    def gather_relay(self, piece, s):
+        @pl.when(direct)
+        def _():
+            self.copy(mine.at[low], mine.at[low], self.gather_send, self.gather_sem.at[4, s], self.far)
+            self.copy(mine.at[high], mine.at[high], self.gather_send, self.gather_sem.at[5, s], self.far)
+
+    def gather_relay(self, piece, s, direct):
         low, high = pl.ds(0, HALF), pl.ds(HALF, HALF)
         left, right = piece(s, self.prev), piece(s, self.next)
         arrived(left.at[low], self.gather_sem.at[0, s])
-        self.copy(left.at[low], left.at[low], self.gather_send, self.gather_sem.at[4, s], self.next)
+
+        @pl.when(jnp.logical_not(direct))
+        def _():
+            self.copy(left.at[low], left.at[low], self.gather_send, self.gather_sem.at[4, s], self.next)
+
         arrived(right.at[high], self.gather_sem.at[1, s])
-        self.copy(right.at[high], right.at[high], self.gather_send, self.gather_sem.at[5, s], self.prev)
+
+        @pl.when(jnp.logical_not(direct))
+        def _():
+            self.copy(right.at[high], right.at[high], self.gather_send, self.gather_sem.at[5, s], self.prev)
 
     def gather_end(self, piece, s):
         low, high = pl.ds(0, HALF), pl.ds(HALF, HALF)
@@ -113,8 +130,6 @@
     turned=pltpu.VMEM((2048, 2048), BF16),
     objective=pltpu.VMEM((2048, K), F32),
     bound=pltpu.VMEM((2048, K), F32),
-    primal=pltpu.VMEM((2048, K), F32),
-    dual=pltpu.VMEM((2048, K), F32),
     extra=pltpu.VMEM((2048, K), BF16),
     dual_bf=pltpu.VMEM((2048, K), BF16),
     lower=pltpu.VMEM((2048, BLOCK), F32),
@@ -129,7 +144,6 @@
     share=pltpu.VMEM((S, K), F32),
     rows=pltpu.VMEM((3, NZ, NX, S, K), BF16),
     core_send=pltpu.VMEM((NJ, NY, S, K), BF16),
-    core_own=pltpu.VMEM((NJ, NY, S, K), F32),
     core_recv=pltpu.VMEM((2, NJ, NY, S, K), BF16),
     part_y=pltpu.VMEM((NJ, NY, S, K), BF16),
     y_from_prev=pltpu.VMEM((2, NJ, S, K), BF16),
@@ -139,16 +153,16 @@
     cols=pltpu.VMEM((2, NJ, NC, NY, S, K), BF16),
     violation=pltpu.VMEM((3, 8, K), F32),
     movement=pltpu.VMEM((3, 8, K), F32),
-    violation_own=pltpu.VMEM((8, K), F32),
-    violation_pair=pltpu.VMEM((8, K), F32),
-    violation_core=pltpu.VMEM((8, K), F32),
-    violation_y=pltpu.VMEM((4, 8, K), F32),
-    movement_own=pltpu.VMEM((8, K), F32),
-    movement_row=pltpu.VMEM((8, K), F32),
-    movement_x=pltpu.VMEM((4, 8, K), F32),
-    movement_z=pltpu.VMEM((8, 8, K), F32),
+    stat_own=pltpu.VMEM((8, K), F32),
+    stat_pair=pltpu.VMEM((8, K), F32),
+    stat_row=pltpu.VMEM((8, K), F32),
+    stat_col=pltpu.VMEM((8, K), F32),
+    stat_core=pltpu.VMEM((8, K), F32),
+    stat_y=pltpu.VMEM((4, 8, K), F32),
+    stat_z=pltpu.VMEM((8, 8, K), F32),
+    stat_x=pltpu.VMEM((4, 8, K), F32),
+    kept=pltpu.VMEM((8, K), F32),
     load_sem=pltpu.SemaphoreType.DMA((16,)),
-    out_sem=pltpu.SemaphoreType.DMA((2,)),
     x_send_sem=pltpu.SemaphoreType.DMA((3,)),
     x_half_prev_sem=pltpu.SemaphoreType.DMA((3, NZ)),
     x_half_next_sem=pltpu.SemaphoreType.DMA((3, NZ)),
@@ -183,9 +197,10 @@
     pass
 
 
-def kernel(constraint, pattern, objective, row_bound, lower, upper, primal_out, dual_out, norms, *refs):
+def kernel(constraint, pattern, objective, row_bound, lower, upper, primal, dual, norms, *refs):
     b = Box()
     b.__dict__.update(zip(SCRATCH, refs))
+    b.primal, b.dual = primal, dual
     y, c, z, x = (lax.axis_index(name) for name in ("y", "c", "z", "x"))
     other = 1 - c
 
@@ -291,22 +306,17 @@
             @pl.when(t < NZ)
             def _():
                 group = z_target(t)
-                if it == 0:
-                    load_matrix(t).wait()
-                    mask_group(group)
                 product = jnp.dot(b.matrix[aligned(group, GROUP)], b.extra[...], preferred_element_type=F32)
                 b.part_x[t] = product.astype(BF16).reshape(NX, S, K)
                 ring.begin(b.part_x, t)
-                if it == 0:
-                    turn_group(group)
-
-            @pl.when((t >= 2) & (t < NZ + 2))
-            def _():
-                ring.relay(b.part_x, t - 2)
-
-            @pl.when(t >= 4)
-            def _():
-                s = t - 4
+
+            @pl.when((t >= LS) & (t < NZ + LS))
+            def _():
+                ring.relay(b.part_x, t - LS)
+
+            @pl.when(t >= 2 * LS)
+            def _():
+                s = t - 2 * LS
                 total = ring.total(b.part_x, s)
 
                 @pl.when(s < NZ - 1)
@@ -320,7 +330,7 @@
 
             return carry
 
-        lax.fori_loop(0, NZ + 4, summing, 0)
+        lax.fori_loop(0, NZ + 2 * LS, summing, 0)
 
         def adding(s, carry):
             arrived(b.z_recv.at[it, s], b.z_recv_sem.at[it, s])
@@ -343,6 +353,10 @@
 
         if it == 0:
             load_bound.wait()
+        if it == ITERS - 1:
+            slack = b.bound[aligned(z * NX + x, S)] - b.share[...]
+            over = jnp.maximum(slack, 0.0)
+            b.violation[it] = folded(over * over)
 
         def gathering(t, carry):
             @pl.when(t < NZ)
@@ -353,20 +367,26 @@
                 def _():
                     arrived(piece(group, x), b.z_gather_sem.at[it, group])
 
-                ring.gather_begin(piece, group)
-
-            @pl.when((t >= 2) & (t < NZ + 2))
-            def _():
-                ring.gather_relay(piece, z_source(t - 2))
-
-            @pl.when(t >= 4)
-            def _():
-                group = z_source(t - 4)
+                ring.gather_begin(piece, group, t >= FAR_X)
+                if it == 0:
+                    turn_group(group)
+
+            if it == ITERS - 1:
+                stats(t)
+
+            @pl.when((t >= LG) & (t < NZ + LG))
+            def _():
+                ring.gather_relay(piece, z_source(t - LG), t - LG >= FAR_X)
+
+            @pl.when(t >= 2 * LG)
+            def _():
+                group = z_source(t - 2 * LG)
                 ring.gather_end(piece, group)
                 at = aligned(group, GROUP)
                 slack = b.bound[at] - rows[group].reshape(GROUP, K).astype(F32)
-                over = jnp.maximum(slack, 0.0)
-                b.violation[it] += folded(over * over)
+                if it < ITERS - 1:
+                    over = jnp.maximum(slack, 0.0)
+                    b.violation[it] += folded(over * over)
                 if it == 0:
                     dual = jnp.maximum(step_dual * slack, 0.0)
                 else:
@@ -374,12 +394,10 @@
                 b.dual[at] = dual
                 if it < ITERS - 1:
                     b.dual_bf[at] = dual.astype(BF16)
-                else:
-                    pltpu.make_async_copy(b.dual.at[at], dual_out.at[at], b.out_sem.at[1]).start()
 
             return carry
 
-        lax.fori_loop(0, NZ + 4, gathering, 0)
+        lax.fori_loop(0, NZ + 2 * LG, gathering, 0)
         ring.drain_sum(b.part_x)
         ring.drain_gather(b.part_x)
         arrived(b.z_send.at[pl.ds(0, NZ - 1)], b.z_send_sem.at[it])
@@ -414,45 +432,45 @@
             def _():
                 b.core_send[t] = product(t, other).astype(BF16).reshape(NY, S, K)
                 swap(b.core_send.at[t], b.core_recv.at[n, t], b.core_send_sem.at[n], b.core_recv_sem.at[n, t])
-                b.core_own[t] = product(t, c).reshape(NY, S, K)
 
             @pl.when((t >= 1) & (t < NJ + 1))
             def _():
                 j = t - 1
+                own = product(j, c).reshape(NY, S, K)
                 arrived(b.core_recv.at[n, j], b.core_recv_sem.at[n, j])
-                b.part_y[j] = (b.core_own[j] + b.core_recv[n, j].astype(F32)).astype(BF16)
+                b.part_y[j] = (own + b.core_recv[n, j].astype(F32)).astype(BF16)
                 ring.begin(b.part_y, j)
 
-            @pl.when((t >= 3) & (t < NJ + 3))
-            def _():
-                ring.relay(b.part_y, t - 3)
-
-            @pl.when((t >= 5) & (t < NJ + 5))
-            def _():
-                j = t - 5
+            @pl.when((t >= 1 + LR) & (t < NJ + 1 + LR))
+            def _():
+                ring.relay(b.part_y, t - 1 - LR)
+
+            @pl.when((t >= 1 + 2 * LR) & (t < NJ + 1 + 2 * LR))
+            def _():
+                j = t - 1 - 2 * LR
                 cols[j, c, y] = ring.total(b.part_y, j).astype(BF16)
-                ring.gather_begin(piece, j)
-
-            @pl.when((t >= 7) & (t < NJ + 7))
-            def _():
-                ring.gather_relay(piece, t - 7)
-
-            @pl.when((t >= 9) & (t < NJ + 9))
-            def _():
-                j = t - 9
+                ring.gather_begin(piece, j, j >= FAR_Y)
+
+            @pl.when((t >= 1 + 3 * LR) & (t < NJ + 1 + 3 * LR))
+            def _():
+                ring.gather_relay(piece, t - 1 - 3 * LR, t - 1 - 3 * LR >= FAR_Y)
+
+            @pl.when((t >= 1 + 4 * LR) & (t < NJ + 1 + 4 * LR))
+            def _():
+                j = t - 1 - 4 * LR
                 ring.gather_end(piece, j)
                 swap(cols.at[j, c], cols.at[j, c], b.core_gather_send.at[n], b.core_gather_sem.at[n, j])
                 update(j, c)
 
-            @pl.when(t >= 10)
-            def _():
-                j = t - 10
+            @pl.when(t >= 2 + 4 * LR)
+            def _():
+                j = t - 2 - 4 * LR
                 arrived(cols.at[j, other], b.core_gather_sem.at[n, j])
                 update(j, other)
 
             return carry
 
-        lax.fori_loop(0, NJ + 10, body, 0)
+        lax.fori_loop(0, NJ + 2 + 4 * LR, body, 0)
         ring.drain_sum(b.part_y)
         ring.drain_gather(b.part_y)
         arrived(b.core_send, b.core_send_sem.at[n])
@@ -463,55 +481,72 @@
             src_ref=src, dst_ref=dst, send_sem=b.stat_send_sem.at[send], recv_sem=recv, device_id=to, device_id_type=MESH
         ).start()
 
-    def three_rows(parts):
-        sums = [jnp.sum(parts[i], axis=0, keepdims=True) for i in range(3)]
-        return jnp.concatenate(sums + [jnp.zeros((5, K), F32)], axis=0)
-
+    def stacked(parts):
+        sums = [jnp.sum(part, axis=0, keepdims=True) for part in parts]
+        return jnp.concatenate(sums + [jnp.zeros((8 - len(parts), K), F32)], axis=0)
+
+    def stats(t):
+        @pl.when(t == 0)
+        def _():
+            b.stat_own[...] = stacked([b.violation[i] for i in range(3)])
+            stat_copy(b.stat_own, b.stat_core, 0, b.stat_c_sem.at[0], {"c": other})
+
+        @pl.when(t == 1)
+        def _():
+            arrived(b.stat_core, b.stat_c_sem.at[0])
+            b.stat_pair[...] = b.stat_own[...] + b.stat_core[...]
+            for step in range(1, NY):
+                stat_copy(b.stat_pair, b.stat_y.at[step], 1, b.stat_y_sem.at[step], {"y": (y + step) % NY})
+
+        @pl.when(t == NZ - 1)
+        def _():
+            total = b.stat_pair[...]
+            for step in range(1, NY):
+                arrived(b.stat_y.at[step], b.stat_y_sem.at[step])
+                total += b.stat_y[step]
+            b.kept[...] = total
+            moved = stacked([b.movement[i] for i in range(3)])
+            b.stat_row[...] = jnp.concatenate([moved[0:3], total[2:3], jnp.zeros((4, K), F32)], axis=0)
+            for step in range(1, NZ):
+                stat_copy(b.stat_row, b.stat_z.at[step], 2, b.stat_z_sem.at[step], {"z": (z + step) % NZ})
+
+        @pl.when(t == NZ + 2 * LG - 2)
+        def _():
+            total = b.stat_row[...]
+            for step in range(1, NZ):
+                arrived(b.stat_z.at[step], b.stat_z_sem.at[step])
+                total += b.stat_z[step]
+            b.stat_col[...] = total
+            for step in range(1, NX):
+                stat_copy(b.stat_col, b.stat_x.at[step], 3, b.stat_x_sem.at[step], {"x": (x + step) % NX})
+
+    def finish_stats():
+        total = b.stat_col[...]
+        for step in range(1, NX):
+            arrived(b.stat_x.at[step], b.stat_x_sem.at[step])
+            total += b.stat_x[step]
+        over = jnp.concatenate([b.kept[0:2], total[3:4]], axis=0)
+        each = jnp.sqrt(over / (2048 * NY * NC) + epsilon) + jnp.sqrt(total[0:3] / (2048 * NZ * NX) + epsilon)
+        norms[...] = each[0:1] + each[1:2] + each[2:3]
+        arrived(b.stat_core, b.stat_send_sem.at[0])
+        arrived(b.stat_y.at[pl.ds(1, 3)], b.stat_send_sem.at[1])
+        arrived(b.stat_z.at[pl.ds(1, 7)], b.stat_send_sem.at[2])
+        arrived(b.stat_x.at[pl.ds(1, 3)], b.stat_send_sem.at[3])
+
+    def prepare(t, carry):
+        load_matrix(t).wait()
+        mask_group(z_target(t))
+        return carry
+
+    lax.fori_loop(0, NZ, prepare, 0)
     pl.semaphore_wait(barrier, peers)
     column_sum(0)
     row_sum(1)
     column_sum(1)
     row_sum(2)
 
-    save_primal = pltpu.make_async_copy(b.primal, primal_out, b.out_sem.at[0])
-    save_primal.start()
-    b.movement_own[...] = three_rows(b.movement)
-    for step in range(1, NX):
-        stat_copy(b.movement_own, b.movement_x.at[step], 0, b.stat_x_sem.at[step], {"x": (x + step) % NX})
-
     column_sum(2)
-
-    b.violation_own[...] = three_rows(b.violation)
-    stat_copy(b.violation_own, b.violation_core, 2, b.stat_c_sem.at[0], {"c": other})
-    row = b.movement_own[...]
-    for step in range(1, NX):
-        arrived(b.movement_x.at[step], b.stat_x_sem.at[step])
-        row += b.movement_x[step]
-    b.movement_row[...] = row
-    for step in range(1, NZ):
-        stat_copy(b.movement_row, b.movement_z.at[step], 1, b.stat_z_sem.at[step], {"z": (z + step) % NZ})
-    arrived(b.violation_core, b.stat_c_sem.at[0])
-    pair = b.violation_own[...] + b.violation_core[...]
-    b.violation_pair[...] = pair
-    for step in range(1, NY):
-        stat_copy(b.violation_pair, b.violation_y.at[step], 3, b.stat_y_sem.at[step], {"y": (y + step) % NY})
-
-    moved = b.movement_row[...]
-    for step in range(1, NZ):
-        arrived(b.movement_z.at[step], b.stat_z_sem.at[step])
-        moved += b.movement_z[step]
-    for step in range(1, NY):
-        arrived(b.violation_y.at[step], b.stat_y_sem.at[step])
-        pair += b.violation_y[step]
-    each = jnp.sqrt(pair / (2048 * NY * NC) + epsilon) + jnp.sqrt(moved / (2048 * NZ * NX) + epsilon)
-    norms[...] = each[0:1] + each[1:2] + each[2:3]
-
-    arrived(b.movement_x.at[pl.ds(1, 3)], b.stat_send_sem.at[0])
-    arrived(b.movement_z.at[pl.ds(1, 7)], b.stat_send_sem.at[1])
-    arrived(b.violation_core, b.stat_send_sem.at[2])
-    arrived(b.violation_y.at[pl.ds(1, 3)], b.stat_send_sem.at[3])
-    save_primal.wait()
-    arrived(b.dual, b.out_sem.at[1])
+    finish_stats()
 
 
 def on_device(constraint, pattern, objective, row_bound, lower_bound, upper_bound):
@@ -523,21 +558,21 @@
             jax.ShapeDtypeStruct((1, K), F32),
         ),
         in_specs=[
-            pl.BlockSpec(memory_space=pl.ANY),
+            pl.BlockSpec(memory_space=pltpu.HBM),
             pl.BlockSpec(memory_space=pltpu.SMEM),
-            pl.BlockSpec(memory_space=pl.ANY),
-            pl.BlockSpec(memory_space=pl.ANY),
+            pl.BlockSpec(memory_space=pltpu.HBM),
+            pl.BlockSpec(memory_space=pltpu.HBM),
             pl.BlockSpec(memory_space=pltpu.VMEM),
             pl.BlockSpec(memory_space=pltpu.VMEM),
         ],
         out_specs=(
-            pl.BlockSpec(memory_space=pl.ANY),
-            pl.BlockSpec(memory_space=pl.ANY),
+            pl.BlockSpec(memory_space=pltpu.VMEM),
+            pl.BlockSpec(memory_space=pltpu.VMEM),
             pl.BlockSpec(memory_space=pltpu.VMEM),
         ),
         scratch_shapes=list(SCRATCH.values()),
         compiler_params=pltpu.CompilerParams(
-            collective_id=0, has_side_effects=True, vmem_limit_bytes=62 * 1024 * 1024
+            collective_id=0, has_side_effects=True, vmem_limit_bytes=48 * 1024 * 1024
         ),
         name="pdhg",
     )(constraint, pattern, objective, row_bound, lower_bound.reshape(16, BLOCK), upper_bound.reshape(16, BLOCK))

time: 183 us -> 154 us (0.84)
  Pallas kernels: 175 us -> 148 us
    pallas_call x1, Pallas kernels: 175 us -> 148 us  [on_device(): pl.pallas_call(kernel, out_shape=(jax.ShapeDtypeStruct((2048, K), F32), j...]
    unnamed x7 -> x9, local copies, waits for them, and re-layouts: 5.08 us -> 5.29 us
where the time goes in v2:
time: 154 us
  Pallas kernels  148 us (96%)
  local copies, waits for them, and re-layouts  5.29 us (3%)
    pallas_call x1, Pallas kernels, on_device(): pl.pallas_call(kernel, out_shape=(jax.ShapeDtypeStruct((2048, K), F32), j...  148 us
    unnamed x9, local copies, waits for them, and re-layouts  5.29 us

profile of v2, /device:TPU:8, one launch (start us, length us, event | category | flops | bytes accessed | tf_op | source)
XLA Modules:
  0.0 153.6 jit_solution(4826669322920614318)
XLA Ops:
  0.6 0.0 copy-start
  0.6 0.7 copy-done
  1.3 0.0 copy-start.1
  1.3 0.7 copy-done.1
  2.0 0.0 copy-start.2
  2.0 0.7 copy-done.2
  2.7 147.7 %pdhg.1 = (f32[2048,256]{1,0:T(8,128)S(1)}, f32[2048,256]{1,0:T(8,128)S(1)}, f32[1,256]{1,0:T(1,128)S(1)}) custom-call(bf16[2048,2048]{1,0:T(8,128)(2,1)} %constraint.1, s32[16,16]{1,0:T(8,128)S(1)} %copy-done, f32[2048,256]{1,0:T(8,128)} %objective.1, f32[2048,256]{1,0:T(8,128)} %row_bound.1, f32[16,128]{1,0:T(8,128)S(1)} %bitcast.3, f32[16,128]{1,0:T(8,128)S(1)} %bitcast.4), custom_call_target="tpu_custom_call" | custom-call | tf_op jit(solution)/shard_map/pdhg/pallas_call | solution.py:553
  150.4 1.3 copy.12
  151.7 1.3 copy.13
  153.0 0.6 copy.14
Async XLA Ops:
  0.6 0.7 copy-start
  1.3 0.7 copy-start.1
  2.0 0.7 copy-start.2

commit v3 on v2

--- a/solution.py
+++ b/solution.py
@@ -59,17 +59,15 @@
         low, high = pl.ds(0, HALF), pl.ds(HALF, HALF)
         self.copy(part.at[s, self.far, low], self.half_prev.at[s], self.send_sem, self.half_prev_sem.at[s], self.next)
         self.copy(part.at[s, self.far, high], self.half_next.at[s], self.send_sem, self.half_next_sem.at[s], self.prev)
-        self.copy(part.at[s, self.next, high], self.from_prev.at[s, high], self.send_sem, self.prev_sem.at[s], self.next)
-        self.copy(part.at[s, self.prev, low], self.from_next.at[s, low], self.send_sem, self.next_sem.at[s], self.prev)
 
     def relay(self, part, s):
         low, high = pl.ds(0, HALF), pl.ds(HALF, HALF)
         arrived(self.half_prev.at[s], self.half_prev_sem.at[s])
         part[s, self.next, low] = (part[s, self.next, low].astype(F32) + self.half_prev[s].astype(F32)).astype(BF16)
-        self.copy(part.at[s, self.next, low], self.from_prev.at[s, low], self.send_sem, self.prev_sem.at[s], self.next)
+        self.copy(part.at[s, self.next], self.from_prev.at[s], self.send_sem, self.prev_sem.at[s], self.next)
         arrived(self.half_next.at[s], self.half_next_sem.at[s])
         part[s, self.prev, high] = (part[s, self.prev, high].astype(F32) + self.half_next[s].astype(F32)).astype(BF16)
-        self.copy(part.at[s, self.prev, high], self.from_next.at[s, high], self.send_sem, self.next_sem.at[s], self.prev)
+        self.copy(part.at[s, self.prev], self.from_next.at[s], self.send_sem, self.next_sem.at[s], self.prev)
 
     def total(self, part, s):
         arrived(self.from_prev.at[s], self.prev_sem.at[s])

time: 154 us -> 152 us (0.987)
  Pallas kernels: 148 us -> 146 us
    pallas_call x1, Pallas kernels: 148 us -> 146 us  [on_device(): pl.pallas_call(kernel, out_shape=(jax.ShapeDtypeStruct((2048, K), F32), j...]
where the time goes in v3:
time: 152 us
  Pallas kernels  146 us (96%)
  local copies, waits for them, and re-layouts  5.29 us (3%)
    pallas_call x1, Pallas kernels, on_device(): pl.pallas_call(kernel, out_shape=(jax.ShapeDtypeStruct((2048, K), F32), j...  146 us
    unnamed x9, local copies, waits for them, and re-layouts  5.29 us

profile of v3, /device:TPU:8, one launch (start us, length us, event | category | flops | bytes accessed | tf_op | source)
XLA Modules:
  0.0 151.7 jit_solution(15054441397818015951)
XLA Ops:
  0.6 0.0 copy-start
  0.6 0.7 copy-done
  1.3 0.0 copy-start.1
  1.3 0.7 copy-done.1
  2.0 0.0 copy-start.2
  2.0 0.7 copy-done.2
  2.7 145.7 %pdhg.1 = (f32[2048,256]{1,0:T(8,128)S(1)}, f32[2048,256]{1,0:T(8,128)S(1)}, f32[1,256]{1,0:T(1,128)S(1)}) custom-call(bf16[2048,2048]{1,0:T(8,128)(2,1)} %constraint.1, s32[16,16]{1,0:T(8,128)S(1)} %copy-done, f32[2048,256]{1,0:T(8,128)} %objective.1, f32[2048,256]{1,0:T(8,128)} %row_bound.1, f32[16,128]{1,0:T(8,128)S(1)} %bitcast.3, f32[16,128]{1,0:T(8,128)S(1)} %bitcast.4), custom_call_target="tpu_custom_call" | custom-call | tf_op jit(solution)/shard_map/pdhg/pallas_call | solution.py:551
  148.5 1.3 copy.12
  149.8 1.3 copy.13
  151.1 0.6 copy.14
Async XLA Ops:
  0.6 0.7 copy-start
  1.3 0.7 copy-start.1
  2.0 0.7 copy-start.2

commit v4 on v3

--- a/solution.py
+++ b/solution.py
@@ -24,8 +24,8 @@
 LS = 4
 LG = 4
 LR = 3
-FAR_X = 6
-FAR_Y = 3
+FAR_X = 5
+FAR_Y = 2
 step_primal = 0.6
 step_dual = 0.6
 epsilon = 1e-6
@@ -283,6 +283,10 @@
                 eye, b.matrix[at, cols], (((1,), (1,)), ((), ())), preferred_element_type=F32
             ).astype(BF16)
 
+    def part_product(t):
+        product = jnp.dot(b.matrix[aligned(z_target(t), GROUP)], b.extra[...], preferred_element_type=F32)
+        b.part_x[t] = product.astype(BF16).reshape(NX, S, K)
+
     def column_sum(it):
         ring = Ring(
             "x", NZ, b.x_from_prev.at[it], b.x_from_next.at[it], b.x_half_prev.at[it], b.x_half_next.at[it],
@@ -303,9 +307,11 @@
         def summing(t, carry):
             @pl.when(t < NZ)
             def _():
-                group = z_target(t)
-                product = jnp.dot(b.matrix[aligned(group, GROUP)], b.extra[...], preferred_element_type=F32)
-                b.part_x[t] = product.astype(BF16).reshape(NX, S, K)
+
+                @pl.when(t > (0 if it == 0 else -1))
+                def _():
+                    part_product(t)
+
                 ring.begin(b.part_x, t)
 
             @pl.when((t >= LS) & (t < NZ + LS))
@@ -537,6 +543,7 @@
         return carry
 
     lax.fori_loop(0, NZ, prepare, 0)
+    part_product(0)
     pl.semaphore_wait(barrier, peers)
     column_sum(0)
     row_sum(1)

time: 152 us -> 152 us (level)
  no operation moved by 1% of the time
where the time goes in v4:
time: 152 us; the launch traced here: 151 us
  Pallas kernels  145 us (95%)
  local copies, waits for them, and re-layouts  5.29 us (3%)
    pallas_call x1, Pallas kernels, on_device(): pl.pallas_call(kernel, out_shape=(jax.ShapeDtypeStruct((2048, K), F32), j...  145 us
    unnamed x9, local copies, waits for them, and re-layouts  5.29 us

profile of v4, /device:TPU:8, one launch (start us, length us, event | category | flops | bytes accessed | tf_op | source)
XLA Modules:
  0.0 150.9 jit_solution(17664108836297055389)
XLA Ops:
  0.6 0.0 copy-start
  0.6 0.7 copy-done
  1.3 0.0 copy-start.1
  1.3 0.7 copy-done.1
  2.0 0.0 copy-start.2
  2.0 0.7 copy-done.2
  2.7 145.0 %pdhg.1 = (f32[2048,256]{1,0:T(8,128)S(1)}, f32[2048,256]{1,0:T(8,128)S(1)}, f32[1,256]{1,0:T(1,128)S(1)}) custom-call(bf16[2048,2048]{1,0:T(8,128)(2,1)} %constraint.1, s32[16,16]{1,0:T(8,128)S(1)} %copy-done, f32[2048,256]{1,0:T(8,128)} %objective.1, f32[2048,256]{1,0:T(8,128)} %row_bound.1, f32[16,128]{1,0:T(8,128)S(1)} %bitcast.3, f32[16,128]{1,0:T(8,128)S(1)} %bitcast.4), custom_call_target="tpu_custom_call" | custom-call | tf_op jit(solution)/shard_map/pdhg/pallas_call | solution.py:558
  147.7 1.3 copy.12
  149.1 1.3 copy.13
  150.4 0.6 copy.14
Async XLA Ops:
  0.6 0.7 copy-start
  1.3 0.7 copy-start.1
  2.0 0.7 copy-start.2
